TPU v7x, 32 devices: a whole 2x2x4 slice. The times are simulated.
32 devices in a mesh: bra: 8 (over z, x), ket: 2 (over y), mpo: 2 (over core).
Axes of the slice: x: 2, y: 2, z: 4, core: 2. Of those that a mesh axis runs over, the one named last changes fastest.
Arguments:
- left_env: bfloat16 [4, 3072, 3072], P('mpo', 'bra', 'ket'), may hold values from -6 to 6
- site_tensor: bfloat16 [3072, 4, 3072], P('bra', None, 'ket'), may hold values from -0.0546875 to 0.0546875
- block_values: float32 [12, 4, 4], replicated, may hold values from -3 to 3
- pair_in: int32 [12], replicated, may hold values from 0 to 3
- pair_out: int32 [12], replicated, may hold values from 0 to 3, as said below
Outputs:
- new_env: bfloat16 [4, 3072, 3072], P('mpo', 'bra', 'ket')
Inputs may be any that keep to these rules, and one draw needn't show every extreme that they name: `pair_out`: every component number 0 to 3 appears at least once.
All inputs are finite; a program needn't handle non-finite values.
Results may differ from a plain program's by a relative error of at most 0.018.
Values may be sent and summed in bfloat16 or wider, within the bound.
A program may use at most 192 MiB of HBM per device.

v0:
```python
import jax
import jax.numpy as jnp
from jax import lax
from jax.sharding import PartitionSpec as P

K = 4


def local(left_env, site_tensor, block_values, pair_in, pair_out):
    comps_loc = left_env.shape[0]
    rows_loc = left_env.shape[1]
    cols_loc = left_env.shape[2]
    phys = site_tensor.shape[1]
    comps = jnp.arange(K, dtype=jnp.int32)
    hot_out = (pair_out[:, None] == comps[None, :]).astype(jnp.float32)
    hot_in = (pair_in[:, None] == comps[None, :]).astype(jnp.float32)
    mixing = jnp.einsum(
        "pv,pw,pst->vswt", hot_out, hot_in, block_values, precision=lax.Precision.HIGHEST
    )
    own_start = lax.axis_index("mpo") * comps_loc
    site_full = lax.all_gather(site_tensor, "bra", axis=0, tiled=True)
    full_rows = site_full.shape[0]
    site_flat = site_full.reshape(full_rows, phys * cols_loc)
    piece = lax.all_gather(left_env, "ket", axis=2, tiled=True)
    width = piece.shape[2]
    panel = site_flat
    half = jnp.dot(
        piece.reshape(comps_loc * rows_loc, width), panel, preferred_element_type=jnp.float32
    )
    half = half.astype(jnp.bfloat16).reshape(comps_loc, rows_loc, phys, cols_loc)
    mix_local = lax.dynamic_slice_in_dim(mixing, own_start, comps_loc, 2)
    contrib = jnp.einsum(
        "vswt,watc->vasc", mix_local, half.astype(jnp.float32), precision=lax.Precision.HIGHEST
    )
    mixed = lax.psum_scatter(contrib.astype(jnp.bfloat16), "mpo", scatter_dimension=0, tiled=True)
    site_wide = lax.all_gather(site_tensor, "ket", axis=2, tiled=True)
    site_pairs = site_wide.reshape(rows_loc * phys, site_wide.shape[2])
    mixed_pairs = mixed.reshape(comps_loc, rows_loc * phys, cols_loc)
    panel = site_pairs
    owned = lax.psum_scatter(
        jnp.einsum("ke,wkc->ewc", panel, mixed_pairs, preferred_element_type=jnp.float32).astype(
            jnp.bfloat16
        ),
        "bra",
        scatter_dimension=0,
        tiled=True,
    ).astype(jnp.float32)
    return jnp.transpose(owned, (1, 0, 2)).astype(jnp.bfloat16)


def solution(mesh):
    return jax.shard_map(
        local,
        mesh=mesh,
        in_specs=(P("mpo", "bra", "ket"), P("bra", None, "ket"), P(), P(), P()),
        out_specs=P("mpo", "bra", "ket"),
        check_vma=False,
    )
```

profile of v0, /device:TPU:0, one launch (start us, length us, event | category | flops | bytes accessed | tf_op | source)
XLA Modules:
  0.0 1338.8 jit_solution(5971266096619716666)
XLA Ops:
  6.5 0.0 copy-start
  6.5 0.7 all-gather.6.cloned.1.call-update
  7.3 0.0 all-gather.4.cloned.1.call-start
  7.3 0.7 all-gather.4.cloned.1.call-update
  8.0 0.0 all-gather.8.cloned.1.call-start
  8.1 5.5 copy.8
  13.5 0.0 all-gather.8.cloned.1.call-update
  13.6 0.0 reduce-scatter.5.cloned.1.call-start
  13.6 0.0 copy-done.2
  13.6 0.0 copy-done.3
  13.6 0.1 fusion.8
  13.7 0.1 multiply_bitcast_fusion
  13.8 0.4 fusion.4
  14.2 713.7 %all-gather.6.cloned.1.call-done = bf16[3072,4,1536]{2,1,0:T(4,128)(2,1)} async-done(((bf16[384,4,1536]{2,1,0:T(4,128)(2,1)}), bf16[3072,4,1536]{2,1,0:T(4,128)(2,1)}) %all-gather.6.cloned.1.call-update) | async-done | bytes 37748752 | tf_op jit(solution)/shard_map/all_gather | solution.py:21
  727.9 27.1 %copy.21 = bf16[384,8,4,1536]{3,1,2,0:T(8,128)(2,1)} copy(bf16[384,8,4,1536]{3,2,1,0:T(4,128)(2,1)} %bitcast.38) | data formatting | bytes 75497472
  755.1 37.0 %all-gather.4.cloned.1.call-done = bf16[2,384,3072]{2,1,0:T(8,128)(2,1)} async-done(((bf16[2,384,1536]{2,1,0:T(8,128)(2,1)}), bf16[2,384,3072]{2,1,0:T(8,128)(2,1)}) %all-gather.4.cloned.1.call-update) | async-done | bytes 4718608 | tf_op jit(solution)/shard_map/all_gather | solution.py:24
  792.1 35.7 %convolution_convert_fusion = bf16[768,6144]{1,0:T(8,128)(2,1)} fusion(bf16[768,3072]{1,0:T(8,128)(2,1)} %bitcast.42, bf16[3072,6144]{1,0:T(8,128)(2,1)} %bitcast.39), kind=kOutput, calls=%fused_computation.3 | convolution fusion | flops 28995747840 | bytes 51904512 | tf_op jit(solution)/shard_map/dot_general | solution.py:27
  827.8 15.3 %reshape.18 = bf16[2,384,4,1536,1]{3,2,1,0,4:T(4,128)(2,1)} reshape(bf16[768,6144]{1,0:T(8,128)(2,1)} %convolution_convert_fusion) | data formatting | bytes 18874368 | tf_op jit(solution)/shard_map/reshape | solution.py:30
  843.1 35.6 %fusion.2 = bf16[384,1536,4,4,1]{1,3,4,2,0:T(4,128)(2,1)} fusion(bf16[2,384,4,1536,1]{3,2,1,0,4:T(4,128)(2,1)} %reshape.18, f32[2,4,4,4]{3,1,2,0:T(4,128)S(1)} %constant_dynamic-slice_fusion), kind=kOutput, calls=%fused_computation.5 | convolution fusion | flops 905969664 | bytes 28312064 | tf_op jit(solution)/shard_map/vswt,watc->vasc/dot_general | solution.py:32
  878.7 31.4 %copy.14 = bf16[384,1536,4,4,1]{0,1,3,2,4:T(8,128)(2,1)} copy(bf16[384,1536,4,4,1]{1,3,4,2,0:T(4,128)(2,1)} %fusion.2) | data formatting | bytes 37748736 | tf_op jit(solution)/shard_map/vswt,watc->vasc/dot_general | solution.py:32
  910.2 17.9 %fusion = bf16[4,384,4,1536]{1,3,2,0:T(8,128)(2,1)} fusion(bf16[384,1536,4,4,1]{0,1,3,2,4:T(8,128)(2,1)} %copy.14), kind=kLoop, calls=%fused_computation.2 | loop fusion | bytes 37748736 | tf_op jit(solution)/shard_map/convert_element_type | solution.py:35
  928.1 0.0 reduce-scatter.5.cloned.1.call-update
  928.1 0.2 reduce-scatter.7.cloned.1.call-start
  928.3 0.0 all-gather.8.cloned.1.call-done
  928.3 26.4 %reduce-scatter.5.cloned.1.call-done = bf16[2,384,4,1536]{1,3,2,0:T(8,128)(2,1)} async-done(((bf16[4,384,4,1536]{1,3,2,0:T(8,128)(2,1)}), bf16[2,384,4,1536]{1,3,2,0:T(8,128)(2,1)}) %reduce-scatter.5.cloned.1.call-update) | async-done | bytes 9437200 | tf_op jit(solution)/shard_map/reduce_scatter | solution.py:35
  954.8 36.2 %bitcast_convert_fusion = bf16[2,1536,3072]{2,1,0:T(8,128)(2,1)} fusion(bf16[2,384,4,1536]{1,3,2,0:T(8,128)(2,1)} %reduce-scatter.5.cloned.1.call-done, bf16[384,4,3072]{2,0,1:T(8,128)(2,1)} %all-gather.8.cloned.1.call-done), kind=kOutput, calls=%fused_computation | convolution fusion | flops 29000466432 | bytes 37748736 | tf_op jit(solution)/shard_map/ke,wkc->ewc/dot_general | solution.py:41
  990.9 24.6 %copy.18 = bf16[3072,3072]{1,0:T(8,128)(2,1)} copy(bf16[3072,3072]{0,1:T(8,128)(2,1)} %bitcast.40) | data formatting | bytes 37748736
  1015.5 0.0 reduce-scatter.7.cloned.1.call-update
  1015.5 0.0 copy-start.1
  1015.5 311.1 %reduce-scatter.7.cloned.1.call-done = bf16[384,3072]{1,0:T(8,128)(2,1)} async-done(((bf16[3072,3072]{1,0:T(8,128)(2,1)}), bf16[384,3072]{1,0:T(8,128)(2,1)}) %reduce-scatter.7.cloned.1.call-update) | async-done | bytes 2359312
  1326.7 3.0 copy.19
  1329.7 2.6 copy.9
  (6 shorter events, 0.0 us)
Async XLA Ops:
  6.5 7.2 copy-start
  6.5 721.4 %all-gather.6.cloned.1.call-start = ((), (), s32[]{:S(2)}) async-start(), calls=%async_computation.3 | async-start | bytes 42467328 | tf_op jit(solution)/shard_map/all_gather | solution.py:21
  7.3 6.3 copy-start.2
  7.3 6.3 copy-start.3
  7.3 784.8 %all-gather.4.cloned.1.call-start = ((), (), s32[]{:S(2)}) async-start(), calls=%async_computation.2 | async-start | bytes 7077888 | tf_op jit(solution)/shard_map/all_gather | solution.py:24
  8.0 920.3 %all-gather.8.cloned.1.call-start = ((), (), s32[]{:S(2)}) async-start(), calls=%async_computation.5 | async-start | bytes 14155776 | tf_op jit(solution)/shard_map/all_gather | solution.py:36
  13.6 941.2 %reduce-scatter.5.cloned.1.call-start = ((), (), s32[]{:S(2)}) async-start(), calls=%async_computation.4 | async-start | bytes 28311552 | tf_op jit(solution)/shard_map/reduce_scatter | solution.py:35
  928.1 398.6 %reduce-scatter.7.cloned.1.call-start = ((), (), s32[]{:S(2)}) async-start(), calls=%async_computation.6 | async-start | bytes 21233664
  1015.5 316.8 %copy-start.1 = (f32[12,4,4]{0,2,1:T(4,128)S(1)}, f32[12,4,4]{0,2,1:T(4,128)}, u32[]{:S(2)}) copy-start(f32[12,4,4]{0,2,1:T(4,128)} %param.7) | copy-start | bytes 2308
Sparse Core Ops, SparseCore 0:
  8.9 719.0 all-gather.5
  729.5 62.5 all-gather.3
  793.7 117.9 all-gather.7
  928.2 26.5 reduce-scatter.4
  1015.6 310.9 reduce-scatter.6
where the time goes:
time: 1340 us
  waiting for transfers between devices  1090 us (81%)
  local copies, waits for them, and re-layouts  127 us (9%)
  matrix products  108 us (8%)
    all_gather x1, waiting for transfers between devices, local(): site_full = lax.all_gather(site_tensor, 'bra', axis=0, tiled=True)  714 us
    unnamed x6, waiting for transfers between devices  313 us
    unnamed x12, local copies, waits for them, and re-layouts  60.2 us
    all_gather x1, waiting for transfers between devices, local(): piece = lax.all_gather(left_env, 'ket', axis=2, tiled=True)  37 us
    dot_general x1, matrix products, local(): jnp.einsum('ke,wkc->ewc', panel, mixed_pairs, preferred_element_type=jnp....  36.2 us
    dot_general x1, matrix products, local(): jnp.dot(piece.reshape(comps_loc * rows_loc, width), panel, preferred_elem...  35.7 us
    dot_general x1, matrix products, local(): jnp.einsum('vswt,watc->vasc', mix_local, half.astype(jnp.float32), precis...  35.6 us
    dot_general x1, local copies, waits for them, and re-layouts, local(): jnp.einsum('vswt,watc->vasc', mix_local, half.astype(jnp.float32), precis...  31.4 us
  transfers between devices with their start and end apart: 5, of which 4 were waited for; matrix products, arithmetic and copies ran while one was open for 13% of the time, Pallas kernels for 0%

commit v1 on v0

v1 whole, which is shorter than its diff:
```python
import jax
import jax.numpy as jnp
from jax import lax
from jax.sharding import PartitionSpec as P

K = 4


def local(left_env, site_tensor, block_values, pair_in, pair_out):
    comps_loc = left_env.shape[0]
    rows_loc = left_env.shape[1]
    cols_loc = left_env.shape[2]
    phys = site_tensor.shape[1]
    comps = jnp.arange(K, dtype=jnp.int32)
    hot_out = (pair_out[:, None] == comps[None, :]).astype(jnp.float32)
    hot_in = (pair_in[:, None] == comps[None, :]).astype(jnp.float32)
    mixing = jnp.einsum(
        "pv,pw,pst->vswt", hot_out, hot_in, block_values, precision=lax.Precision.HIGHEST
    )
    splits = lax.axis_size("mpo")
    half_cols = cols_loc // splits
    own_start = lax.axis_index("mpo") * half_cols
    site_own = lax.dynamic_slice_in_dim(site_tensor, own_start, half_cols, 2)
    site_full = lax.all_gather(
        site_own.reshape(rows_loc, phys * half_cols), "bra", axis=0, tiled=True
    )
    piece = lax.all_gather(left_env, "ket", axis=2, tiled=True)
    piece = lax.all_gather(piece, "mpo", axis=0, tiled=True)
    comps_all, width = piece.shape[0], piece.shape[2]
    half = jnp.dot(
        piece.reshape(comps_all * rows_loc, width), site_full, preferred_element_type=jnp.float32
    )
    half = half.astype(jnp.bfloat16).reshape(comps_all, rows_loc, phys, half_cols)
    mixed = jnp.einsum(
        "vswt,watc->savc", mixing, half.astype(jnp.float32), precision=lax.Precision.HIGHEST
    ).astype(jnp.bfloat16)
    mixed_pairs = mixed.reshape(phys * rows_loc, comps_all * half_cols)
    site_wide = lax.all_gather(
        jnp.transpose(site_tensor, (1, 0, 2)), "ket", axis=2, tiled=True
    )
    site_pairs = site_wide.reshape(phys * rows_loc, site_wide.shape[2])
    term = lax.dot_general(
        site_pairs, mixed_pairs, (((0,), (0,)), ((), ())), preferred_element_type=jnp.float32
    ).astype(jnp.bfloat16)
    owned = lax.psum_scatter(term, "bra", scatter_dimension=0, tiled=True)
    owned = jnp.transpose(owned.reshape(-1, comps_all, half_cols), (1, 0, 2))
    return lax.all_to_all(owned, "mpo", split_axis=0, concat_axis=2, tiled=True)


def solution(mesh):
    return jax.shard_map(
        local,
        mesh=mesh,
        in_specs=(P("mpo", "bra", "ket"), P("bra", None, "ket"), P(), P(), P()),
        out_specs=P("mpo", "bra", "ket"),
        check_vma=False,
    )
```

time: 1340 us -> 980 us (0.73)
  waiting for transfers between devices: 1090 us -> 766 us
  local copies, waits for them, and re-layouts: 127 us -> 98 us
  matrix products: 108 us -> 93.9 us
    all_gather x2 -> x3, waiting for transfers between devices: 714 us -> 389 us  [the longest x1 365 us: local(): lax.all_gather(site_own.reshape(rows_loc, phys * half_cols), 'bra', axis=...]
    dot_general x1 -> x0, local copies, waits for them, and re-layouts: 31.4 us -> none  [local(): jnp.einsum('vswt,watc->vasc', mix_local, half.astype(jnp.float32), precis...]
    all_gather x1, waiting for transfers between devices: 37 us -> 67 us  [local(): piece = lax.all_gather(left_env, 'ket', axis=2, tiled=True)]
    reduce_scatter x1 -> x0, waiting for transfers between devices: 26.4 us -> none  [local(): lax.psum_scatter(contrib.astype(jnp.bfloat16), 'mpo', scatter_dimension=0...]
    reshape x1 -> x2, local copies, waits for them, and re-layouts: 15.3 us -> 35.7 us  [local(): half.astype(jnp.bfloat16).reshape(comps_all, rows_loc, phys, half_cols)]
    unnamed x12 -> x11, local copies, waits for them, and re-layouts: 60.2 us -> 44.8 us
    convert_element_type x2 -> x1, local copies, waits for them, and re-layouts: 20.5 us -> 6.24 us  [local(): mixed = jnp.einsum('vswt,watc->savc', mixing, half.astype(jnp.float32), p...]
    dot_general x3, matrix products: 107 us -> 93.6 us  [the longest x1 36.8 us: local(): lax.dot_general(site_pairs, mixed_pairs, (((0,), (0,)), ((), ())), prefer...]
  transfers between devices with their start and end apart: 5 -> 5, of which waited for: 4 -> 5; matrix products, arithmetic and copies ran while one was open for 13% -> 12% of each run, Pallas kernels for 0% -> 0%
where the time goes in v1:
time: 980 us; the launch traced here: 978 us
  waiting for transfers between devices  766 us (78%)
  local copies, waits for them, and re-layouts  98 us (10%)
  matrix products  93.9 us (10%)
  between operations  13.2 us (1%)
    all_gather x1, waiting for transfers between devices, local(): lax.all_gather(site_own.reshape(rows_loc, phys * half_cols), 'bra', axis=...  365 us
    unnamed x6, waiting for transfers between devices  311 us
    all_gather x1, waiting for transfers between devices, local(): piece = lax.all_gather(left_env, 'ket', axis=2, tiled=True)  67 us
    unnamed x11, local copies, waits for them, and re-layouts  44.8 us
    dot_general x1, matrix products, local(): lax.dot_general(site_pairs, mixed_pairs, (((0,), (0,)), ((), ())), prefer...  36.8 us
    dot_general x1, matrix products, local(): jnp.dot(piece.reshape(comps_all * rows_loc, width), site_full, preferred_...  36.7 us
    reshape x2, local copies, waits for them, and re-layouts, local(): half.astype(jnp.bfloat16).reshape(comps_all, rows_loc, phys, half_cols)  35.7 us
    dot_general x1, matrix products, local(): jnp.einsum('vswt,watc->savc', mixing, half.astype(jnp.float32), precision...  20.1 us
  transfers between devices with their start and end apart: 5, of which 5 were waited for; matrix products, arithmetic and copies ran while one was open for 12% of the time, Pallas kernels for 0%

profile of v1, /device:TPU:0, one launch (start us, length us, event | category | flops | bytes accessed | tf_op | source)
XLA Modules:
  0.0 978.1 jit_solution(10487822228750793544)
XLA Ops:
  6.5 0.7 all-gather.7.cloned.1.call-update
  7.3 0.0 all-gather.9.cloned.1.call-start
  7.3 67.0 %all-gather.7.cloned.1.call-done = bf16[2,384,3072]{2,1,0:T(8,128)(2,1)} async-done(((bf16[2,384,1536]{2,1,0:T(8,128)(2,1)}), bf16[2,384,3072]{2,1,0:T(8,128)(2,1)}) %all-gather.7.cloned.1.call-update) | async-done | bytes 4718608 | tf_op jit(solution)/shard_map/all_gather | solution.py:27
  74.3 0.0 all-gather.9.cloned.1.call-update
  74.3 0.0 all-gather.5.cloned.1.call-start
  74.3 2.5 constant_dynamic-slice_fusion
  76.8 1.9 copy.27
  78.7 0.0 all-gather.5.cloned.1.call-update
  78.7 0.0 all-gather.11.cloned.1.call-start
  78.8 5.8 copy.34
  84.5 0.0 all-gather.11.cloned.1.call-update
  84.6 0.0 reduce-scatter.4.cloned.1.call-start
  84.6 0.0 copy-done.1
  84.6 0.0 copy-done.2
  84.7 0.3 convolution_bitcast_fusion
  85.0 12.5 %all-gather.9.cloned.1.call-done = bf16[4,384,3072]{2,1,0:T(8,128)(2,1)} async-done(((bf16[2,384,3072]{2,1,0:T(8,128)(2,1)}), bf16[4,384,3072]{2,1,0:T(8,128)(2,1)}) %all-gather.9.cloned.1.call-update) | async-done | bytes 9437200 | tf_op jit(solution)/shard_map/all_gather | solution.py:28
  97.5 365.1 %all-gather.5.cloned.1.call-done = bf16[3072,3072]{1,0:T(8,128)(2,1)} async-done(((bf16[384,3072]{1,0:T(8,128)(2,1)}), bf16[3072,3072]{1,0:T(8,128)(2,1)}) %all-gather.5.cloned.1.call-update) | async-done | bytes 18874384 | tf_op jit(solution)/shard_map/all_gather | solution.py:24
  462.6 36.7 %fusion = bf16[1536,3072]{0,1:T(8,128)(2,1)} fusion(bf16[3072,3072]{1,0:T(8,128)(2,1)} %all-gather.5.cloned.1.call-done, bf16[1536,3072]{1,0:T(8,128)(2,1)} %bitcast.57), kind=kOutput, calls=%fused_computation.3 | convolution fusion | flops 28995747840 | bytes 37748736 | tf_op jit(solution)/shard_map/dot_general | solution.py:30
  499.3 16.5 %reshape.22 = bf16[4,384,4,768]{1,0,3,2:T(4,128)(2,1)} reshape(bf16[1536,3072]{0,1:T(8,128)(2,1)} %fusion) | data formatting | bytes 18874368 | tf_op jit(solution)/shard_map/reshape | solution.py:33
  515.8 19.3 %copy.19 = bf16[4,384,4,768,1]{3,0,2,4,1:T(4,128)(2,1)} copy(bf16[4,384,4,768,1]{1,0,3,2,4:T(4,128)(2,1)} %bitcast.48) | data formatting | bytes 18874368 | tf_op jit(solution)/shard_map/reshape | solution.py:33
  535.0 20.1 %fusion.1 = bf16[4,384,4,768]{3,0,2,1:T(4,128)(2,1)S(1)} fusion(bf16[4,384,4,768,1]{3,0,2,4,1:T(4,128)(2,1)} %copy.19, f32[4,4,4,4,1]{1,2,3,0,4:T(4,128)S(1)} %convolution_bitcast_fusion), kind=kOutput, calls=%fused_computation.4 | convolution fusion | flops 910688256 | bytes 18875392 | tf_op jit(solution)/shard_map/vswt,watc->savc/dot_general | solution.py:34
  555.2 6.2 copy.15
  561.4 9.6 copy.28
  571.0 11.0 %all-gather.11.cloned.1.call-done = bf16[4,384,3072]{2,1,0:T(8,128)(2,1)} async-done(((bf16[4,384,1536]{2,1,0:T(8,128)(2,1)}), bf16[4,384,3072]{2,1,0:T(8,128)(2,1)}) %all-gather.11.cloned.1.call-update) | async-done | bytes 9437200 | tf_op jit(solution)/shard_map/all_gather | solution.py:38
  582.0 36.8 %convert_bitcast_fusion = bf16[3072,3072]{0,1:T(8,128)(2,1)} fusion(bf16[1536,3072]{1,0:T(8,128)(2,1)} %bitcast.51, bf16[1536,3072]{1,0:T(8,128)(2,1)} %bitcast.58), kind=kOutput, calls=%fused_computation.1 | convolution fusion | flops 29000466432 | bytes 37748736 | tf_op jit(solution)/shard_map/dot_general | solution.py:42
  618.8 24.6 %copy.25 = bf16[3072,3072]{1,0:T(8,128)(2,1)} copy(bf16[3072,3072]{0,1:T(8,128)(2,1)} %convert_bitcast_fusion) | data formatting | bytes 37748736
  643.4 0.0 reduce-scatter.4.cloned.1.call-update
  643.4 309.9 %reduce-scatter.4.cloned.1.call-done = bf16[384,3072]{1,0:T(8,128)(2,1)} async-done(((bf16[3072,3072]{1,0:T(8,128)(2,1)}), bf16[384,3072]{1,0:T(8,128)(2,1)}) %reduce-scatter.4.cloned.1.call-update) | async-done | bytes 2359312
  953.3 3.0 copy.26
  956.3 6.5 all_to_all.18
  962.9 6.0 copy.17
  968.8 2.8 all_to_all.16
  (6 shorter events, 0.0 us)
Async XLA Ops:
  6.5 67.7 %all-gather.7.cloned.1.call-start = ((), (), s32[]{:S(2)}) async-start(), calls=%async_computation.3 | async-start | bytes 7077888 | tf_op jit(solution)/shard_map/all_gather | solution.py:27
  7.3 90.2 %all-gather.9.cloned.1.call-start = ((), (), s32[]{:S(2)}) async-start(), calls=%async_computation.4 | async-start | bytes 14155776 | tf_op jit(solution)/shard_map/all_gather | solution.py:28
  74.3 388.3 %all-gather.5.cloned.1.call-start = ((), (), s32[]{:S(2)}) async-start(), calls=%async_computation.2 | async-start | bytes 21233664 | tf_op jit(solution)/shard_map/all_gather | solution.py:24
  78.7 5.9 copy-start.1
  78.7 5.9 copy-start.2
  78.7 5.9 copy-start
  78.7 503.3 %all-gather.11.cloned.1.call-start = ((), (), s32[]{:S(2)}) async-start(), calls=%async_computation.5 | async-start | bytes 14155776 | tf_op jit(solution)/shard_map/all_gather | solution.py:38
  84.6 868.7 %reduce-scatter.4.cloned.1.call-start = ((), (), s32[]{:S(2)}) async-start(), calls=%async_computation.6 | async-start | bytes 21233664
Sparse Core Ops, SparseCore 0:
  8.9 65.3 all-gather.6
  75.8 21.6 all-gather.8
  99.0 363.5 all-gather.4
  464.0 117.9 all-gather.10
  643.5 309.7 reduce-scatter.3
